TPU v7x, 32 devices: a 4x4x1 block of a 4x4x8 slice. The times are simulated.
32 devices in a mesh: dp: 1 (over z), heads: 4 (over y), ctx: 8 (over x, core).
Axes of the slice: x: 4, y: 4, z: 1, core: 2. Of those that a mesh axis runs over, the one named last changes fastest.
The devices are a block of a 4x4x8 slice.
Arguments:
- hidden: bfloat16 [512, 5120], P(('dp', 'ctx'))
- w_query: bfloat16 [5120, 4096], P(None, 'heads')
- w_key: bfloat16 [5120, 1024], P(None, 'heads')
- w_value: bfloat16 [5120, 1024], P(None, 'heads')
- w_out: bfloat16 [4096, 5120], P('heads')
- prefix_k: bfloat16 [8192, 8, 128], P(('dp', 'ctx'), 'heads')
- prefix_v: bfloat16 [8192, 8, 128], P(('dp', 'ctx'), 'heads')
- suffix_k: bfloat16 [512, 512, 8, 128], P(('dp', 'ctx'), None, 'heads')
- suffix_v: bfloat16 [512, 512, 8, 128], P(('dp', 'ctx'), None, 'heads')
- seq_lens: int32 [512], P(('dp', 'ctx'))
Outputs:
- output: bfloat16 [512, 5120], P(('dp', 'ctx'))
All inputs are finite; a program needn't handle non-finite values.
Results may differ from a plain program's by a relative error of at most 0.00452898.
Values are sent between devices in bfloat16 or wider.
A program may use at most 768 MiB of HBM per device.

v0:
```python
import functools
import jax
import jax.numpy as jnp
from jax import lax
from jax.sharding import PartitionSpec as P


def prefix_state(q_block, pre_k, pre_v):
    score_scale = q_block.shape[-1] ** -0.5
    scores = jnp.einsum('bkgd,pkd->bkgp', q_block, pre_k, preferred_element_type=jnp.float32) * score_scale
    row_max = jnp.max(scores, axis=-1)
    weights = jnp.exp(scores - row_max[..., None])
    weight_sum = jnp.sum(weights, axis=-1)
    summed = jnp.einsum('bkgp,pkd->bkgd', weights.astype(jnp.bfloat16), pre_v, preferred_element_type=jnp.float32)
    return summed / weight_sum[..., None], row_max + jnp.log(weight_sum)


def suffix_state(queries, key_new, val_new, suf_k, suf_v, seq_lens):
    score_scale = queries.shape[-1] ** -0.5
    cached = jnp.einsum('bkgd,bskd->bkgs', queries, suf_k, preferred_element_type=jnp.float32) * score_scale
    slot_ids = jnp.arange(suf_k.shape[1])
    in_range = (slot_ids[None, :] < seq_lens[:, None])[:, None, None, :]
    cached = jnp.where(in_range, cached, -jnp.inf)
    new_score = jnp.einsum('clhe,cle->clh', queries, key_new, preferred_element_type=jnp.float32) * score_scale
    row_max = jnp.maximum(jnp.max(cached, axis=-1), new_score)
    w_cached = jnp.exp(cached - row_max[..., None])
    w_fresh = jnp.exp(new_score - row_max)
    weight_sum = jnp.sum(w_cached, axis=-1) + w_fresh
    summed = jnp.einsum('bkgs,bskd->bkgd', w_cached.astype(jnp.bfloat16), suf_v, preferred_element_type=jnp.float32)
    summed = summed + jnp.einsum('clh,cle->clhe', w_fresh.astype(jnp.bfloat16), val_new, preferred_element_type=jnp.float32)
    return summed / weight_sum[..., None], row_max + jnp.log(weight_sum)


def merge_states(pre_out, pre_lse, suf_out, suf_lse):
    all_max = jnp.maximum(jnp.max(pre_lse, axis=0), suf_lse)
    pre_w = jnp.exp(pre_lse - all_max)
    suf_w = jnp.exp(suf_lse - all_max)
    norm_sum = jnp.sum(pre_w, axis=0) + suf_w
    merged = jnp.sum(pre_w[..., None] * pre_out, axis=0) + suf_w[..., None] * suf_out
    return merged / norm_sum[..., None]


def solution(mesh):
    row_spec = P(('dp', 'ctx'), None)
    col_spec = P(None, 'heads')
    pre_spec = P(('dp', 'ctx'), 'heads', None)
    suf_spec = P(('dp', 'ctx'), None, 'heads', None)

    def local_step(hidden, w_query, w_key, w_value, w_out, prefix_k, prefix_v, suffix_k, suffix_v, seq_lens):
        n_rows = hidden.shape[0]
        kv_local = prefix_k.shape[1]
        head_dim = prefix_k.shape[2]
        q_group = w_query.shape[1] // (kv_local * head_dim)
        queries = jnp.dot(hidden, w_query, preferred_element_type=jnp.float32).astype(jnp.bfloat16).reshape(n_rows, kv_local, q_group, head_dim)
        key_new = jnp.dot(hidden, w_key, preferred_element_type=jnp.float32).astype(jnp.bfloat16).reshape(n_rows, kv_local, head_dim)
        val_new = jnp.dot(hidden, w_value, preferred_element_type=jnp.float32).astype(jnp.bfloat16).reshape(n_rows, kv_local, head_dim)
        all_queries = lax.all_gather(queries, 'ctx', axis=0)
        pre_out, pre_lse = lax.map(functools.partial(prefix_state, pre_k=prefix_k, pre_v=prefix_v), all_queries)
        pre_out = lax.all_to_all(pre_out, 'ctx', 0, 0, tiled=True)
        pre_lse = lax.all_to_all(pre_lse, 'ctx', 0, 0, tiled=True)
        suf_out, suf_lse = suffix_state(queries, key_new, val_new, suffix_k, suffix_v, seq_lens)
        merged = merge_states(pre_out, pre_lse, suf_out, suf_lse)
        attended = merged.astype(jnp.bfloat16).reshape(n_rows, kv_local * q_group * head_dim)
        partial_y = jnp.dot(attended, w_out, preferred_element_type=jnp.float32)
        summed_y = lax.psum(partial_y, 'heads')
        return (hidden.astype(jnp.float32) + summed_y).astype(jnp.bfloat16)

    return jax.shard_map(local_step, mesh=mesh, in_specs=(row_spec, col_spec, col_spec, col_spec, P('heads', None), pre_spec, pre_spec, suf_spec, suf_spec, P(('dp', 'ctx'))), out_specs=row_spec, check_vma=False)
```

profile of v0, /device:TPU:97, one launch (start us, length us, event | category | flops | bytes accessed | tf_op | source)
XLA Modules:
  0.0 180.9 jit_solution(8256319910391189795)
XLA Ops:
  6.6 6.3 %convolution_convert_fusion = bf16[64,1024]{1,0:T(8,128)(2,1)S(1)} fusion(bf16[64,5120]{1,0:T(8,128)(2,1)} %param.12, bf16[5120,1024]{1,0:T(8,128)(2,1)} %param.13), kind=kOutput, calls=%fused_computation.27 | convolution fusion | flops 671154176 | bytes 11272192 | tf_op jit(solution)/shard_map/dot_general | solution.py:54
  13.7 1.1 copy.29
  14.9 1.9 %copy.30 = bf16[1024,2,128]{2,0,1:T(8,128)(2,1)} copy(bf16[1024,2,128]{2,1,0:T(2,128)(2,1)} %param.18) | data formatting | bytes 1048576 | tf_op jit(solution)/shard_map/while | solution.py:58
  16.9 21.8 %all-gather.2.cloned.1.call-done = bf16[8,64,2,4,128]{4,1,3,2,0:T(8,128)(2,1)} async-done(((bf16[1,64,2,4,128]{4,1,3,2,0:T(8,128)(2,1)}), bf16[8,64,2,4,128]{4,1,3,2,0:T(8,128)(2,1)}) %all-gather.2.cloned.1.call-update) | async-done | bytes 1048592 | tf_op jit(solution)/shard_map/all_gather | solution.py:57
  38.6 26.7 %while.12 = (s32[]{:T(128)}, f32[8,64,2,4,128]{4,1,3,2,0:T(8,128)}, f32[8,64,2,4]{1,3,2,0:T(4,128)S(1)}, bf16[8,64,2,4,128]{4,1,3,2,0:T(8,128)(2,1)}, bf16[1024,...) while((s32[]{:T(128)}, f32[8,64,2,4,128]{4,1,3,2,0:T(8,128)}, ...), condition=%wide.region_3.4_spmd, body=%wide.region_0.3_spmd.sunk | while | flops 272694784 | bytes 9853053 | solution.py:58
  38.6 1.5 bitcast_reduce_fusion.3
  40.6 1.3 fusion.77
  42.0 1.5 bitcast_reduce_fusion.3
  44.0 1.3 fusion.77
  45.3 1.5 bitcast_reduce_fusion.3
  47.4 1.3 fusion.77
  48.7 1.5 bitcast_reduce_fusion.3
  50.7 1.3 fusion.77
  52.0 1.5 bitcast_reduce_fusion.3
  54.1 1.3 fusion.77
  55.4 1.5 bitcast_reduce_fusion.3
  57.4 1.3 fusion.77
  58.7 1.5 bitcast_reduce_fusion.3
  60.7 1.3 fusion.77
  62.0 1.5 bitcast_reduce_fusion.3
  64.1 1.3 fusion.77
  66.1 3.5 %all-to-all-start = ((f32[8,1,512]{2,1,0:T(1,128)}), f32[8,1,512]{2,1,0:T(1,128)S(1)}, u32[]{:S(2)}, u32[]{:S(2)}) async-start(f32[8,1,512]{2,1,0:T(1,128)} %reshape.66), calls=%async_computation | async-start | bytes 32768 | tf_op jit(solution)/shard_map/all_to_all | solution.py:60
  69.6 11.9 %fusion.56 = (f32[64,2,4]{2,1,0:T(2,128)}, f32[64,2,4,512]{3,2,1,0:T(4,128)}) fusion(bf16[64,2,4,128]{3,2,1,0:T(4,128)(2,1)S(1)} %reshape.55, bf16[64,512,2,128]{3,2,1,0:T(2,128)(2,1)} %param.19, pred[64,512]{1,0:T(8,128)(4,1)S(1)} %iota_compare_fusion), kind=kOutput, calls=%fused_computation.53 | convolution fusion | flops 67894784 | bytes 17991680 | tf_op jit(solution)/shard_map/bkgd,bskd->bkgs/dot_general | solution.py:20
  81.4 5.0 %all-to-all-start.1 = ((f32[8,64,2,4,128]{4,1,3,2,0:T(8,128)}), f32[8,64,2,4,128]{4,1,3,2,0:T(8,128)}, u32[]{:S(2)}, u32[]{:S(2)}) async-start(f32[8,64,2,4,128]{4,1,3,2,0:T(8,128)} %get-tuple-element.39), calls=%async_computation.1 | async-start | bytes 4194304 | tf_op jit(solution)/shard_map/all_to_all | solution.py:59
  89.9 1.9 %fusion.46 = f32[64,2,4]{2,1,0:T(2,128)S(1)} fusion(f32[64,2,4,512]{3,2,1,0:T(4,128)} %get-tuple-element.81, f32[64,2,4]{2,1,0:T(2,128)S(1)} %copy.33), kind=kLoop, calls=%fused_computation.39 | loop fusion | flops 523776 | bytes 1052672 | tf_op jit(solution)/shard_map/reduce_sum | solution.py:28
  91.9 2.3 %fusion.29 = f32[64,256]{1,0:T(8,128)S(1)} fusion(bf16[64,5120]{1,0:T(8,128)(2,1)S(1)} %copy-done.1, bf16[5120,256]{1,0:T(8,128)(2,1)} %param.15), kind=kOutput, calls=%fused_computation.30 | convolution fusion | flops 167804928 | bytes 3342336 | tf_op jit(solution)/shard_map/dot_general | solution.py:56
  99.2 13.3 %all-to-all-done.1 = f32[8,64,2,4,128]{4,1,3,2,0:T(8,128)} async-done(((f32[8,64,2,4,128]{4,1,3,2,0:T(8,128)}), f32[8,64,2,4,128]{4,1,3,2,0:T(8,128)}, u32[]{:S(2)}, u32[]{:S(2)}) %all-to-all-start.1) | async-done | bytes 2097184 | tf_op jit(solution)/shard_map/all_to_all | solution.py:59
  112.6 2.0 %multiply_reduce_fusion = f32[64,2,4,128]{3,0,2,1:T(8,128)S(1)} fusion(f32[8,64,2,4,128]{4,1,3,2,0:T(8,128)} %all-to-all-done.1, f32[8,64,2,4]{1,3,2,0:T(4,128)S(1)} %get-tuple-element.75), kind=kLoop, calls=%fused_computation.23 | loop fusion | flops 983040 | bytes 2375680 | tf_op jit(solution)/shard_map/reduce_sum | solution.py:39
  114.7 8.3 %fusion.42 = bf16[64,2,4,128]{3,2,1,0:T(4,128)(2,1)S(1)} fusion(bf16[64,512,2,128]{3,2,1,0:T(2,128)(2,1)} %param.20, f32[64,2,4,512]{3,2,1,0:T(4,128)S(1)} %copy-done.2, f32[64,2,4]{2,1,0:T(2,128)S(1)} %copy.33, f32[64,2,4,128]{3,0,2,1:T(8,128)S(1)} %multiply_reduce_fusion, f32[64,2,4]{2,1,0:T(2,128)S(1)} %copy-done.7, f32[64,2,4]{2,1,0:T(2,128)S(1)} %copy-done.6, ...), kind=kOutput, calls=%fused_computation.37 | convolution fusion | flops 68091904 | bytes 18294784 | tf_op jit(solution)/shard_map/bkgs,bskd->bkgd/dot_general | solution.py:29
  123.1 7.0 %fusion.58 = f32[64,5120]{1,0:T(8,128)} fusion(bf16[64,1024]{1,0:T(8,128)(2,1)S(1)} %reshape.58, bf16[1024,5120]{1,0:T(8,128)(2,1)} %param.16), kind=kOutput, calls=%fused_computation.56 | convolution fusion | flops 671088640 | bytes 11927552 | tf_op jit(solution)/shard_map/dot_general | solution.py:64
  130.1 41.7 %all-reduce.2.cloned.1.call-done = f32[64,5120]{1,0:T(8,128)} async-done(((f32[64,5120]{1,0:T(8,128)}), f32[64,5120]{1,0:T(8,128)}) %all-reduce.2.cloned.1.call-update) | async-done | bytes 1310736 | tf_op jit(solution)/shard_map/psum | solution.py:65
  171.8 2.3 %add_convert_fusion = bf16[64,5120]{1,0:T(8,128)(2,1)} fusion(f32[64,5120]{1,0:T(8,128)} %all-reduce.2.cloned.1.call-done, bf16[64,5120]{1,0:T(8,128)(2,1)S(1)} %copy-done.1), kind=kLoop, calls=%fused_computation.24 | loop fusion | flops 983040 | bytes 2621440 | tf_op jit(solution)/shard_map/convert_element_type | solution.py:66
  (83 shorter events, 14.7 us)
Async XLA Ops:
  6.5 79.9 %copy-start = (bf16[5120,256]{1,0:T(8,128)(2,1)S(1)}, bf16[5120,256]{1,0:T(8,128)(2,1)}, u32[]{:S(2)}) copy-start(bf16[5120,256]{1,0:T(8,128)(2,1)} %param.14) | copy-start | bytes 7864324
  6.6 32.1 %all-gather.2.cloned.1.call-start = ((), (), s32[]{:S(2)}) async-start(), calls=%async_computation.2 | async-start | bytes 1179648 | tf_op jit(solution)/shard_map/all_gather | solution.py:57
  12.8 3.9 %copy-start.9 = (s32[64]{0:T(128)S(1)}, s32[64]{0:T(128)}, u32[]{:S(2)}) copy-start(s32[64]{0:T(128)} %param.21) | copy-start | bytes 772
  38.6 2.0 %copy-start.3 = (bf16[1024,2,128]{2,0,1:T(8,128)(2,1)S(1)}, bf16[1024,2,128]{2,0,1:T(8,128)(2,1)}, u32[]{:S(2)}) copy-start(bf16[1024,2,128]{2,0,1:T(8,128)(2,1)} %get-tuple-element.144) | copy-start | bytes 1572868 | tf_op jit(solution)/shard_map/while
  42.0 2.0 %copy-start.3 = (bf16[1024,2,128]{2,0,1:T(8,128)(2,1)S(1)}, bf16[1024,2,128]{2,0,1:T(8,128)(2,1)}, u32[]{:S(2)}) copy-start(bf16[1024,2,128]{2,0,1:T(8,128)(2,1)} %get-tuple-element.144) | copy-start | bytes 1572868 | tf_op jit(solution)/shard_map/while
  45.3 2.0 %copy-start.3 = (bf16[1024,2,128]{2,0,1:T(8,128)(2,1)S(1)}, bf16[1024,2,128]{2,0,1:T(8,128)(2,1)}, u32[]{:S(2)}) copy-start(bf16[1024,2,128]{2,0,1:T(8,128)(2,1)} %get-tuple-element.144) | copy-start | bytes 1572868 | tf_op jit(solution)/shard_map/while
  48.7 2.0 %copy-start.3 = (bf16[1024,2,128]{2,0,1:T(8,128)(2,1)S(1)}, bf16[1024,2,128]{2,0,1:T(8,128)(2,1)}, u32[]{:S(2)}) copy-start(bf16[1024,2,128]{2,0,1:T(8,128)(2,1)} %get-tuple-element.144) | copy-start | bytes 1572868 | tf_op jit(solution)/shard_map/while
  52.0 2.0 %copy-start.3 = (bf16[1024,2,128]{2,0,1:T(8,128)(2,1)S(1)}, bf16[1024,2,128]{2,0,1:T(8,128)(2,1)}, u32[]{:S(2)}) copy-start(bf16[1024,2,128]{2,0,1:T(8,128)(2,1)} %get-tuple-element.144) | copy-start | bytes 1572868 | tf_op jit(solution)/shard_map/while
  55.4 2.0 %copy-start.3 = (bf16[1024,2,128]{2,0,1:T(8,128)(2,1)S(1)}, bf16[1024,2,128]{2,0,1:T(8,128)(2,1)}, u32[]{:S(2)}) copy-start(bf16[1024,2,128]{2,0,1:T(8,128)(2,1)} %get-tuple-element.144) | copy-start | bytes 1572868 | tf_op jit(solution)/shard_map/while
  58.7 2.0 %copy-start.3 = (bf16[1024,2,128]{2,0,1:T(8,128)(2,1)S(1)}, bf16[1024,2,128]{2,0,1:T(8,128)(2,1)}, u32[]{:S(2)}) copy-start(bf16[1024,2,128]{2,0,1:T(8,128)(2,1)} %get-tuple-element.144) | copy-start | bytes 1572868 | tf_op jit(solution)/shard_map/while
  62.0 2.0 %copy-start.3 = (bf16[1024,2,128]{2,0,1:T(8,128)(2,1)S(1)}, bf16[1024,2,128]{2,0,1:T(8,128)(2,1)}, u32[]{:S(2)}) copy-start(bf16[1024,2,128]{2,0,1:T(8,128)(2,1)} %get-tuple-element.144) | copy-start | bytes 1572868 | tf_op jit(solution)/shard_map/while
  66.1 15.4 %all-to-all-start = ((f32[8,1,512]{2,1,0:T(1,128)}), f32[8,1,512]{2,1,0:T(1,128)S(1)}, u32[]{:S(2)}, u32[]{:S(2)}) async-start(f32[8,1,512]{2,1,0:T(1,128)} %reshape.66), calls=%async_computation | async-start | bytes 32768 | tf_op jit(solution)/shard_map/all_to_all | solution.py:60
  81.4 5.0 %copy-start.1 = (bf16[64,5120]{1,0:T(8,128)(2,1)S(1)}, bf16[64,5120]{1,0:T(8,128)(2,1)}, u32[]{:S(2)}) copy-start(bf16[64,5120]{1,0:T(8,128)(2,1)} %param.12) | copy-start | bytes 1966084
  81.4 31.1 %all-to-all-start.1 = ((f32[8,64,2,4,128]{4,1,3,2,0:T(8,128)}), f32[8,64,2,4,128]{4,1,3,2,0:T(8,128)}, u32[]{:S(2)}, u32[]{:S(2)}) async-start(f32[8,64,2,4,128]{4,1,3,2,0:T(8,128)} %get-tuple-element.39), calls=%async_computation.1 | async-start | bytes 4194304 | tf_op jit(solution)/shard_map/all_to_all | solution.py:59
  86.5 85.4 %all-reduce.2.cloned.1.call-start = ((), (), s32[]{:S(2)}) async-start(), calls=%async_computation.3 | async-start | bytes 2621440 | tf_op jit(solution)/shard_map/psum | solution.py:65
  112.6 2.1 %copy-start.2 = (f32[64,2,4,512]{3,2,1,0:T(4,128)S(1)}, f32[64,2,4,512]{3,2,1,0:T(4,128)}, u32[]{:S(2)}) copy-start(f32[64,2,4,512]{3,2,1,0:T(4,128)} %get-tuple-element.81) | copy-start | bytes 3145732
  112.6 2.1 %copy-start.4 = (f32[64,2,128]{2,1,0:T(2,128)S(1)}, f32[64,2,128]{2,1,0:T(2,128)}, u32[]{:S(2)}) copy-start(f32[64,2,128]{2,1,0:T(2,128)} %reshape.59) | copy-start | bytes 196612
  112.6 2.1 %copy-start.5 = (f32[64,2,4]{2,1,0:T(2,128)S(1)}, f32[64,2,4]{2,1,0:T(2,128)}, u32[]{:S(2)}) copy-start(f32[64,2,4]{2,1,0:T(2,128)} %copy.37) | copy-start | bytes 6148
  112.6 2.1 %copy-start.6 = (f32[64,2,4]{2,1,0:T(2,128)S(1)}, f32[64,2,4]{2,1,0:T(2,128)}, u32[]{:S(2)}) copy-start(f32[64,2,4]{2,1,0:T(2,128)} %copy.38) | copy-start | bytes 6148
  112.6 2.1 %copy-start.7 = (f32[64,2,4]{2,1,0:T(2,128)S(1)}, f32[64,2,4]{2,1,0:T(2,128)}, u32[]{:S(2)}) copy-start(f32[64,2,4]{2,1,0:T(2,128)} %copy.40) | copy-start | bytes 6148
  112.6 2.1 %copy-start.8 = (f32[64,2,4]{2,1,0:T(2,128)S(1)}, f32[64,2,4]{2,1,0:T(2,128)}, u32[]{:S(2)}) copy-start(f32[64,2,4]{2,1,0:T(2,128)} %copy.35) | copy-start | bytes 6148
Sparse Core Ops, SparseCore 0:
  13.8 24.8 all-gather.1
  130.3 41.5 all-reduce.1
where the time goes:
time: 182 us; the launch traced here: 181 us
  waiting for transfers between devices  76.9 us (42%)
  matrix products  59.4 us (33%)
  between operations  13.6 us (7%)
  other arithmetic  11.4 us (6%)
  local copies, waits for them, and re-layouts  11 us (6%)
  starting transfers between devices  8.54 us (5%)
    psum x1, waiting for transfers between devices, local_step(): summed_y = lax.psum(partial_y, 'heads')  41.7 us
    all_gather x1, waiting for transfers between devices, local_step(): all_queries = lax.all_gather(queries, 'ctx', axis=0)  21.8 us
    all_to_all x1, waiting for transfers between devices, local_step(): pre_out = lax.all_to_all(pre_out, 'ctx', 0, 0, tiled=True)  13.3 us
    dot_general x1, matrix products, suffix_state(): jnp.einsum('bkgd,bskd->bkgs', queries, suf_k, preferred_element_type=jnp....  11.9 us
    dot_general x8, matrix products, prefix_state(): jnp.einsum('bkgd,pkd->bkgp', q_block, pre_k, preferred_element_type=jnp.f...  11.8 us
    dot_general x8, matrix products, prefix_state(): jnp.einsum('bkgp,pkd->bkgd', weights.astype(jnp.bfloat16), pre_v, preferr...  10.4 us
    dot_general x1, matrix products, suffix_state(): jnp.einsum('bkgs,bskd->bkgd', w_cached.astype(jnp.bfloat16), suf_v, prefe...  8.3 us
    dot_general x1, matrix products, local_step(): partial_y = jnp.dot(attended, w_out, preferred_element_type=jnp.float32)  7.01 us
  transfers between devices with their start and end apart: 4, of which 3 were waited for; matrix products, arithmetic and copies ran while one was open for 15% of the time, Pallas kernels for 0%

commit v1 on v0

v1 whole, which is shorter than its diff:
```python
import functools
import math
import jax
import jax.numpy as jnp
from jax import lax
from jax.experimental import pallas as pl
from jax.experimental.pallas import tpu as pltpu
from jax.sharding import PartitionSpec as P

MESH = pl.DeviceIdType.MESH
F32 = jnp.float32
BF16 = jnp.bfloat16
LOW = -3.0e38
SEQ_CHUNK = 8
RING = 5
POS_CHUNK = 512


def dot_nt(a, b):
    return lax.dot_general(a, b, (((1,), (1,)), ((), ())), preferred_element_type=F32)


def dot_nn(a, b):
    return lax.dot_general(a, b, (((1,), (0,)), ((), ())), preferred_element_type=F32)


def pack_stats(row_max, row_sum):
    rows = row_max.shape[0]
    lane = lax.broadcasted_iota(jnp.int32, (rows, 128), 1)
    both = jnp.where(lane == 0, row_max, jnp.where(lane == 1, row_sum, 0.0))
    return jnp.transpose(both)[:8]


def unpack_stats(packed):
    rows = packed.shape[1]
    both = jnp.transpose(jnp.concatenate([packed, jnp.zeros((120, rows), F32)], axis=0))
    return both[:, 0:1], both[:, 1:2]


def merge(one, two):
    (num_a, max_a, sum_a), (num_b, max_b, sum_b) = one, two
    top = jnp.maximum(max_a, max_b)
    fac_a, fac_b = jnp.exp2(max_a - top), jnp.exp2(max_b - top)
    return num_a * fac_a + num_b * fac_b, top, sum_a * fac_a + sum_b * fac_b


def kernel(dims, hid_h, wq_h, wk_h, wv_h, wo_h, pk_h, pv_h, sk_h, sv_h, lens, out_h,
           hid, wq, wk, wv, wo, raw, flat, kpre, vpre, qg, q8, knew, vnew,
           ring_k, ring_v, scores, own_num, own_max, own_sum, hold_num, hold_max, hold_sum,
           so8, sm8, sl8, xs_num, xs_st, xr_num, xr_st, att, ys, yr, yblk, ygat,
           s_hid, s_wq, s_wkv, s_wo, s_raw, s_rawsend, s_rawrecv, s_ring,
           s_qs, s_qr, s_xs, s_xr, s_xst, s_xrt, s_ys, s_yr, s_gs, s_gr, s_out):
    n_ctx, n_y, kv_n, grp = dims
    rows = hid.shape[0]
    width = hid.shape[1]
    head = kpre.shape[-1]
    per_kv = grp * head
    heads = kv_n * grp
    local_pos = raw.shape[2] // kv_n
    scale = head ** -0.5 * math.log2(math.e)
    blk = width // n_y
    half = blk // 2

    ctx = lax.axis_index('ctx')
    ypos = lax.axis_index('heads')
    right = {'ctx': lax.rem(ctx + 2, n_ctx)}
    left = {'ctx': lax.rem(ctx + n_ctx - 2, n_ctx)}
    partner = {'ctx': ctx + 1 - 2 * lax.rem(ctx, 2)}
    up = {'heads': lax.rem(ypos + 1, n_y)}
    down = {'heads': lax.rem(ypos + n_y - 1, n_y)}

    def remote(src, dst, send, recv, where):
        return pltpu.make_async_remote_copy(src_ref=src, dst_ref=dst, send_sem=send, recv_sem=recv,
                                            device_id=where, device_id_type=MESH)

    c_hid = pltpu.make_async_copy(hid_h, hid, s_hid)
    c_hid.start()
    n_q = heads // 2
    c_wq = [pltpu.make_async_copy(wq_h.at[:, pl.ds(i * 2 * head, 2 * head)], wq.at[i], s_wq.at[i]) for i in range(n_q)]
    c_raw = [pltpu.make_async_copy(src, raw.at[0, i], s_raw.at[i]) for i, src in enumerate((pk_h, pv_h))]
    c_wq[0].start()
    for c in c_raw:
        c.start()
    for c in c_wq[1:]:
        c.start()

    barrier = pltpu.get_barrier_semaphore()
    for where in (partner, left, right, up, down):
        pl.semaphore_signal(barrier, inc=1, device_id=where, device_id_type=MESH)
    pl.semaphore_wait(barrier, 5)

    c_swap = [remote(src, raw.at[1, i], s_rawsend.at[i], s_rawrecv.at[i], partner) for i, src in enumerate((pk_h, pv_h))]
    for c in c_swap:
        c.start()
    c_wkv = [pltpu.make_async_copy(src, dst, s_wkv.at[i]) for i, (src, dst) in enumerate(((wk_h, wk), (wv_h, wv)))]
    for c in c_wkv:
        c.start()

    def deinterleave(which):
        for i, dst in enumerate((kpre, vpre)):
            flat[...] = raw[which, i].astype(F32)
            for kv in range(kv_n):
                dst[kv, pl.ds(which * local_pos, local_pos), :] = flat[pl.ds(kv, local_pos, stride=kv_n), :].astype(BF16)

    def ring_copies(chunk, slot):
        seqs = pl.ds(chunk * SEQ_CHUNK, SEQ_CHUNK)
        return (pltpu.make_async_copy(sk_h.at[seqs], ring_k.at[slot], s_ring.at[slot, 0]),
                pltpu.make_async_copy(sv_h.at[seqs], ring_v.at[slot], s_ring.at[slot, 1]))

    n_chunks = rows // SEQ_CHUNK

    for c in c_raw:
        c.wait()
    deinterleave(0)

    c_hid.wait()
    q_copies = []
    for kv in range(kv_n):
        for j in range(grp // 2):
            i = kv * (grp // 2) + j
            c_wq[i].wait()
            part = dot_nn(hid[...], wq[i]).astype(BF16)
            qg[0, kv, :, pl.ds(j * 2 * head, 2 * head)] = part
            for g in range(2):
                h = kv * grp + j * 2 + g
                q8[pl.ds(h, rows, stride=heads), :] = part[:, g * head:(g + 1) * head].astype(F32)
        to_right = remote(qg.at[0, kv], qg.at[1, kv], s_qs.at[0, kv], s_qr.at[1, kv], right)
        to_left = remote(qg.at[0, kv], qg.at[2, kv], s_qs.at[1, kv], s_qr.at[2, kv], left)
        to_right.start()
        to_left.start()
        q_copies.append((to_right, to_left))
        if kv == 0:
            for chunk in range(RING):
                for c in ring_copies(chunk, chunk):
                    c.start()
    c_wo = []
    for r in range(2 * n_y):
        dest = lax.rem(ypos + r // 2, n_y)
        col = pl.multiple_of(dest * blk + (r % 2) * half, 128)
        c_wo.append(pltpu.make_async_copy(wo_h.at[:, pl.ds(col, half)], wo.at[r], s_wo.at[r]))
    for c in c_wo:
        c.start()

    for c in c_wkv:
        c.wait()
    knew[...] = dot_nn(hid[...], wk[...]).astype(BF16).astype(F32)
    vnew[...] = dot_nn(hid[...], wv[...]).astype(BF16).astype(F32)

    for c in c_swap:
        c.wait()
    deinterleave(1)

    n_pos = kpre.shape[1]

    def prefix_part(slot, kv):
        queries = jnp.concatenate([qg[slot, kv, :, pl.ds(g * head, head)] for g in range(grp)], axis=0)
        run = None
        for c in range(n_pos // POS_CHUNK):
            at = pl.ds(c * POS_CHUNK, POS_CHUNK)
            s = dot_nt(queries, kpre[kv, at, :])
            scores[:, at] = s
            for t in range(POS_CHUNK // 128):
                piece = s[:, t * 128:(t + 1) * 128]
                run = piece if run is None else jnp.maximum(run, piece)
        row_max = jnp.max(run, axis=1, keepdims=True) * scale
        wide_max = jnp.broadcast_to(row_max, (grp * rows, 128))
        wide_max = jnp.concatenate([wide_max] * (POS_CHUNK // 128), axis=1)
        total, num = None, None
        for c in range(n_pos // POS_CHUNK):
            at = pl.ds(c * POS_CHUNK, POS_CHUNK)
            p = jnp.exp2(scores[:, at] * scale - wide_max)
            for t in range(POS_CHUNK // 128):
                piece = p[:, t * 128:(t + 1) * 128]
                total = piece if total is None else total + piece
            term = dot_nn(p.astype(BF16), vpre[kv, at, :])
            num = term if num is None else num + term
        return num, row_max, jnp.sum(total, axis=1, keepdims=True)

    def post(state, i, where):
        xs_num[i] = state[0]
        xs_st[i] = pack_stats(state[1], state[2])
        out = (remote(xs_num.at[i], xr_num.at[i], s_xs.at[i], s_xr.at[i], where),
               remote(xs_st.at[i], xr_st.at[i], s_xst.at[i], s_xrt.at[i], where))
        for c in out:
            c.start()
        return out

    def received(i, where):
        for c in (remote(xs_num.at[i], xr_num.at[i], s_xs.at[i], s_xr.at[i], where),
                  remote(xs_st.at[i], xr_st.at[i], s_xst.at[i], s_xrt.at[i], where)):
            c.wait_recv()
        return (xr_num[i],) + unpack_stats(xr_st[i])

    def suffix_chunks(first, last):
        lane = lax.broadcasted_iota(jnp.int32, (heads, ring_k.shape[2]), 1)
        line = lax.broadcasted_iota(jnp.int32, (heads, ring_k.shape[2]), 0)
        mine = lax.rem(lane, kv_n) == line // grp
        place = jnp.where(mine, lane // kv_n, ring_k.shape[2])

        @pl.loop(first, last)
        def _(chunk):
            slot = lax.rem(chunk, RING)
            for c in ring_copies(chunk, slot):
                c.wait()
            for i in range(SEQ_CHUNK):
                b = chunk * SEQ_CHUNK + i
                at = pl.ds(pl.multiple_of(b * heads, heads), heads)
                qb = q8[at, :].astype(BF16)
                s = dot_nt(qb, ring_k[slot, i]) * scale
                s = jnp.where(place < lens[b], s, -jnp.inf)
                m = jnp.maximum(jnp.max(s, axis=1, keepdims=True), LOW)
                p = jnp.exp2(s - m)
                so8[at, :] = dot_nn(p.astype(BF16), ring_v[slot, i])
                sm8[at, :] = jnp.broadcast_to(m, (heads, head))
                sl8[at, :] = jnp.broadcast_to(jnp.sum(p, axis=1, keepdims=True), (heads, head))

            @pl.when(chunk + RING < n_chunks)
            def _():
                for c in ring_copies(chunk + RING, slot):
                    c.start()

    def keep(refs, i, state):
        for ref, val in zip(refs, state):
            ref[i] = val if val.shape == ref.shape[1:] else jnp.broadcast_to(val, ref.shape[1:])

    def kept(refs, i):
        return refs[0][i], refs[1][i][:, 0:1], refs[2][i][:, 0:1]

    own = (own_num, own_max, own_sum)
    hold = (hold_num, hold_max, hold_sum)

    keep(own, 0, prefix_part(0, 0))
    q_copies[0][0].wait_recv()
    fwd_right = remote(qg.at[1, 0], qg.at[3, 0], s_qs.at[2, 0], s_qr.at[3, 0], right)
    fwd_right.start()
    keep(own, 1, prefix_part(0, 1))
    q_copies[1][1].wait_recv()
    fwd_left = remote(qg.at[2, 1], qg.at[3, 1], s_qs.at[2, 1], s_qr.at[3, 1], left)
    fwd_left.start()

    sent = []
    q_copies[1][0].wait_recv()
    q_copies[0][1].wait_recv()
    sent += post(prefix_part(2, 1), 0, right)
    sent += post(prefix_part(1, 0), 1, left)
    fwd_right.wait_recv()
    sent += post(prefix_part(3, 0), 2, right)
    fwd_left.wait_recv()
    sent += post(prefix_part(3, 1), 3, left)
    keep(hold, 0, prefix_part(2, 0))
    keep(hold, 1, prefix_part(1, 1))
    suffix_chunks(0, 2)
    sent += post(merge(received(2, right), kept(hold, 0)), 4, right)
    sent += post(merge(received(3, left), kept(hold, 1)), 5, left)
    suffix_chunks(2, n_chunks)

    for kv in range(kv_n):
        states = [kept(own, kv)]
        if kv == 0:
            states += [received(1, left), received(4, right)]
        else:
            states += [received(0, right), received(5, left)]
        state = functools.reduce(merge, states)
        for g in range(grp):
            h = kv * grp + g
            at = slice(g * rows, (g + 1) * rows)
            every = pl.ds(h, rows, stride=heads)
            qh = q8[every, :]
            kn = knew[:, kv * head:(kv + 1) * head]
            vn = vnew[:, kv * head:(kv + 1) * head]
            s_new = jnp.sum(qh * kn, axis=1, keepdims=True) * scale
            full = merge((state[0][at], state[1][at], state[2][at]), (so8[every, :], sm8[every, :], sl8[every, :]))
            full = merge(full, (vn, s_new, jnp.ones_like(s_new)))
            att[:, h * head:(h + 1) * head] = (full[0] / full[2]).astype(BF16)

    ysent = []

    def y_part(r):
        c_wo[r].wait()
        return dot_nn(att[...], wo[r])

    def y_copy(i, where):
        return remote(ys.at[i], yr.at[i], s_ys.at[i], s_yr.at[i], where)

    def y_post(val, i, where):
        ys[i] = val
        c = y_copy(i, where)
        c.start()
        ysent.append(c)

    far, near_up, near_down = 2 * (n_y // 2), 2, 2 * (n_y - 1)
    y_post(y_part(far), 0, up)
    y_post(y_part(far + 1), 1, down)
    y_post(y_part(near_up + 1), 2, up)
    y_post(y_part(near_down), 3, down)
    part_up = y_part(near_up)
    part_down = y_part(near_down + 1)
    y_copy(0, up).wait_recv()
    y_post(part_up + yr[0], 4, up)
    y_copy(1, down).wait_recv()
    y_post(part_down + yr[1], 5, down)
    low, high = y_part(0), y_part(1)
    me_col = pl.multiple_of(ypos * blk, 128)
    y_copy(3, down).wait_recv()
    low = low + yr[3]
    y_copy(2, up).wait_recv()
    high = high + yr[2]
    y_copy(4, up).wait_recv()
    low = low + yr[4] + hid[:, pl.ds(me_col, half)].astype(F32)
    yblk[0] = low.astype(BF16)
    y_copy(5, down).wait_recv()
    high = high + yr[5] + hid[:, pl.ds(pl.multiple_of(me_col + half, 128), half)].astype(F32)
    yblk[1] = high.astype(BF16)

    gsend = []

    def g_copy(src, slot, part, sem, where):
        c = remote(src, ygat.at[slot, part], s_gs.at[sem], s_gr.at[slot, part], where)
        gsend.append(c)
        return c

    g_up = [g_copy(yblk.at[p], 0, p, p, up) for p in range(2)]
    g_down = [g_copy(yblk.at[p], 1, p, 2 + p, down) for p in range(2)]
    for p in range(2):
        g_up[p].start()
        g_down[1 - p].start()

    outs = []

    def put(src, dest, part):
        col = pl.multiple_of(dest * blk + part * half, 128)
        c = pltpu.make_async_copy(src, out_h.at[:, pl.ds(col, half)], s_out.at[len(outs)])
        c.start()
        outs.append(c)

    put(yblk.at[0], ypos, 0)
    put(yblk.at[1], ypos, 1)
    g_up[0].wait_recv()
    f_up = g_copy(ygat.at[0, 0], 2, 0, 4, up)
    f_up.start()
    g_down[1].wait_recv()
    f_down = g_copy(ygat.at[1, 1], 2, 1, 5, down)
    f_down.start()
    below, above = lax.rem(ypos + n_y - 1, n_y), lax.rem(ypos + 1, n_y)
    put(ygat.at[0, 0], below, 0)
    put(ygat.at[1, 1], above, 1)
    g_up[1].wait_recv()
    put(ygat.at[0, 1], below, 1)
    g_down[0].wait_recv()
    put(ygat.at[1, 0], above, 0)
    opposite = lax.rem(ypos + n_y // 2, n_y)
    f_up.wait_recv()
    put(ygat.at[2, 0], opposite, 0)
    f_down.wait_recv()
    put(ygat.at[2, 1], opposite, 1)

    for pair in q_copies:
        for c in pair:
            c.wait_send()
    for c in [fwd_right, fwd_left] + sent + ysent + gsend:
        c.wait_send()
    for c in outs:
        c.wait()


def solution(mesh):
    n_ctx, n_y = mesh.shape['ctx'], mesh.shape['heads']
    row_spec = P(('dp', 'ctx'), None)
    col_spec = P(None, 'heads')
    pre_spec = P(('dp', 'ctx'), 'heads', None)
    suf_spec = P(('dp', 'ctx'), None, 'heads', None)

    def local_step(hidden, w_query, w_key, w_value, w_out, prefix_k, prefix_v, suffix_k, suffix_v, seq_lens):
        rows, width = hidden.shape
        pos, kv_n, head = prefix_k.shape
        slots = suffix_k.shape[1]
        grp = w_query.shape[1] // (kv_n * head)
        heads = kv_n * grp
        blk = width // n_y
        stack = grp * rows
        dma = pltpu.SemaphoreType.DMA
        scratch = dict(
            hid=pltpu.VMEM((rows, width), BF16),
            wq=pltpu.VMEM((heads // 2, width, 2 * head), BF16),
            wk=pltpu.VMEM((width, kv_n * head), BF16),
            wv=pltpu.VMEM((width, kv_n * head), BF16),
            wo=pltpu.VMEM((2 * n_y, heads * head, blk // 2), BF16),
            raw=pltpu.VMEM((2, 2, pos * kv_n, head), BF16),
            flat=pltpu.VMEM((pos * kv_n, head), F32),
            kpre=pltpu.VMEM((kv_n, 2 * pos, head), BF16),
            vpre=pltpu.VMEM((kv_n, 2 * pos, head), BF16),
            qg=pltpu.VMEM((4, kv_n, rows, grp * head), BF16),
            q8=pltpu.VMEM((rows * heads, head), F32),
            knew=pltpu.VMEM((rows, kv_n * head), F32),
            vnew=pltpu.VMEM((rows, kv_n * head), F32),
            ring_k=pltpu.VMEM((RING, SEQ_CHUNK, slots * kv_n, head), BF16),
            ring_v=pltpu.VMEM((RING, SEQ_CHUNK, slots * kv_n, head), BF16),
            scores=pltpu.VMEM((stack, 2 * pos), F32),
            own_num=pltpu.VMEM((kv_n, stack, head), F32),
            own_max=pltpu.VMEM((kv_n, stack, 128), F32),
            own_sum=pltpu.VMEM((kv_n, stack, 128), F32),
            hold_num=pltpu.VMEM((2, stack, head), F32),
            hold_max=pltpu.VMEM((2, stack, 128), F32),
            hold_sum=pltpu.VMEM((2, stack, 128), F32),
            so8=pltpu.VMEM((rows * heads, head), F32),
            sm8=pltpu.VMEM((rows * heads, head), F32),
            sl8=pltpu.VMEM((rows * heads, head), F32),
            xs_num=pltpu.VMEM((6, stack, head), F32),
            xs_st=pltpu.VMEM((6, 8, stack), F32),
            xr_num=pltpu.VMEM((6, stack, head), F32),
            xr_st=pltpu.VMEM((6, 8, stack), F32),
            att=pltpu.VMEM((rows, heads * head), BF16),
            ys=pltpu.VMEM((6, rows, blk // 2), F32),
            yr=pltpu.VMEM((6, rows, blk // 2), F32),
            yblk=pltpu.VMEM((2, rows, blk // 2), BF16),
            ygat=pltpu.VMEM((3, 2, rows, blk // 2), BF16),
            s_hid=dma(()), s_wq=dma((heads // 2,)), s_wkv=dma((2,)), s_wo=dma((2 * n_y,)),
            s_raw=dma((2,)), s_rawsend=dma((2,)), s_rawrecv=dma((2,)), s_ring=dma((RING, 2)),
            s_qs=dma((3, kv_n)), s_qr=dma((4, kv_n)),
            s_xs=dma((6,)), s_xr=dma((6,)), s_xst=dma((6,)), s_xrt=dma((6,)),
            s_ys=dma((6,)), s_yr=dma((6,)), s_gs=dma((6,)), s_gr=dma((3, 2)), s_out=dma((8,)),
        )
        hbm = pl.BlockSpec(memory_space=pl.ANY)
        return pl.pallas_call(
            functools.partial(kernel, (n_ctx, n_y, kv_n, grp)),
            out_shape=jax.ShapeDtypeStruct((rows, width), BF16),
            in_specs=[hbm] * 9 + [pl.BlockSpec(memory_space=pltpu.SMEM)],
            out_specs=hbm,
            scratch_shapes=list(scratch.values()),
            compiler_params=pltpu.CompilerParams(collective_id=0, has_side_effects=True, vmem_limit_bytes=67043328),
        )(hidden, w_query, w_key, w_value, w_out,
          prefix_k.reshape(pos * kv_n, head), prefix_v.reshape(pos * kv_n, head),
          suffix_k.reshape(rows, slots * kv_n, head), suffix_v.reshape(rows, slots * kv_n, head), seq_lens)

    return jax.shard_map(local_step, mesh=mesh, in_specs=(row_spec, col_spec, col_spec, col_spec, P('heads', None), pre_spec, pre_spec, suf_spec, suf_spec, P(('dp', 'ctx'))), out_specs=row_spec, check_vma=False)
```

time: 182 us -> 69.3 us (0.38)
  the two profiles are of different devices: /device:TPU:97 before, /device:TPU:96 now
where the time goes in v1:
time: 69.3 us; the launch traced here: 69.1 us
  Pallas kernels  67.2 us (97%)
  local copies, waits for them, and re-layouts  1.97 us (3%)
    pallas_call x1, Pallas kernels, local_step(): pl.pallas_call(functools.partial(kernel, (n_ctx, n_y, kv_n, grp)), out_sh...  67.2 us
    unnamed x1, local copies, waits for them, and re-layouts  1.97 us

profile of v1, /device:TPU:96, one launch (start us, length us, event | category | flops | bytes accessed | tf_op | source)
XLA Modules:
  0.0 69.1 jit_solution(16382914518438648324)
XLA Ops:
  0.0 67.2 %shard_map.100 = bf16[64,5120]{1,0:T(8,128)(2,1)} custom-call(bf16[64,5120]{1,0:T(8,128)(2,1)} %hid_h.1, bf16[5120,1024]{1,0:T(8,128)(2,1)} %wq_h.1, bf16[5120,256]{1,0:T(8,128)(2,1)} %wk_h.1, bf16[5120,256]{1,0:T(8,128)(2,1)} %wv_h.1, bf16[1024,5120]{1,0:T(8,128)(2,1)} %wo_h.1, bf16[2048,128]{1,0:T(8,128)(2,1)} %bitcast.6, bf16[2048,128]{1,0:T(8,128)(2,1)} %bitcast.7, ...), custom_call_target="tpu_custom_call" | custom-call | tf_op jit(solution)/shard_map/pallas_call | solution.py:424
  67.2 2.0 %copy.12 = bf16[64,5120]{1,0:T(8,128)(2,1)} copy(bf16[64,5120]{1,0:T(8,128)(2,1)} %shard_map.100) | data formatting | bytes 1310720

commit v2 on v0

v2 whole, which is shorter than its diff:
```python
import functools
import math
import jax
import jax.numpy as jnp
from jax import lax
from jax.experimental import pallas as pl
from jax.experimental.pallas import tpu as pltpu
from jax.sharding import PartitionSpec as P

MESH = pl.DeviceIdType.MESH
F32 = jnp.float32
BF16 = jnp.bfloat16
LOW = -3.0e38
GROUP = 16
RING = 2
POS_CHUNK = 512


def dot_nt(a, b):
    return lax.dot_general(a, b, (((1,), (1,)), ((), ())), preferred_element_type=F32)


def dot_nn(a, b):
    return lax.dot_general(a, b, (((1,), (0,)), ((), ())), preferred_element_type=F32)


def pack_stats(row_max, row_sum):
    rows = row_max.shape[0]
    lane = lax.broadcasted_iota(jnp.int32, (rows, 128), 1)
    both = jnp.where(lane == 0, row_max, jnp.where(lane == 1, row_sum, 0.0))
    return jnp.transpose(both)[:8]


def unpack_stats(packed):
    rows = packed.shape[1]
    both = jnp.transpose(jnp.concatenate([packed, jnp.zeros((120, rows), F32)], axis=0))
    return both[:, 0:1], both[:, 1:2]


def merge(one, two):
    (num_a, max_a, sum_a), (num_b, max_b, sum_b) = one, two
    top = jnp.maximum(max_a, max_b)
    fac_a, fac_b = jnp.exp2(max_a - top), jnp.exp2(max_b - top)
    return num_a * fac_a + num_b * fac_b, top, sum_a * fac_a + sum_b * fac_b


def kernel(dims, hid_h, wq_h, wk_h, wv_h, wo_h, pk_h, pv_h, sk_h, sv_h, lens, out_h,
           hid, wq, wk, wv, wo, raw, flat, kpre, vpre, qg, q8, knew, vnew,
           ring_k, ring_v, qbd, sufs, sufp, scores, own_num, own_st, hold_num, hold_st,
           so8, sst8, xs_num, xs_st, xr_num, xr_st, att, yhold, ys, yr, yblk, ygat,
           s_hid, s_wq, s_wkv, s_wo, s_raw, s_rawsend, s_rawrecv, s_ring,
           s_qs, s_qr, s_xs, s_xr, s_xst, s_xrt, s_ys, s_yr, s_gs, s_gr, s_out):
    n_ctx, n_y, kv_n, grp = dims
    rows = hid.shape[0]
    width = hid.shape[1]
    head = kpre.shape[-1]
    heads = kv_n * grp
    local_pos = raw.shape[2] // kv_n
    scale = head ** -0.5 * math.log2(math.e)
    blk = width // n_y
    half = blk // 2
    part_rows = rows // 2
    stack = grp * part_rows

    ctx = lax.axis_index('ctx')
    ypos = lax.axis_index('heads')
    right = {'ctx': lax.rem(ctx + 2, n_ctx)}
    left = {'ctx': lax.rem(ctx + n_ctx - 2, n_ctx)}
    partner = {'ctx': ctx + 1 - 2 * lax.rem(ctx, 2)}
    up = {'heads': lax.rem(ypos + 1, n_y)}
    down = {'heads': lax.rem(ypos + n_y - 1, n_y)}
    below, above, opposite = lax.rem(ypos + n_y - 1, n_y), lax.rem(ypos + 1, n_y), lax.rem(ypos + n_y // 2, n_y)

    def remote(src, dst, send, recv, where):
        return pltpu.make_async_remote_copy(src_ref=src, dst_ref=dst, send_sem=send, recv_sem=recv,
                                            device_id=where, device_id_type=MESH)

    c_hid = pltpu.make_async_copy(hid_h, hid, s_hid)
    c_raw = [pltpu.make_async_copy(src, raw.at[0, i], s_raw.at[i]) for i, src in enumerate((pk_h, pv_h))]
    c_wq = [pltpu.make_async_copy(wq_h.at[:, pl.ds(kv * grp * head, grp * head)], wq.at[kv], s_wq.at[kv]) for kv in range(kv_n)]
    c_wkv = [pltpu.make_async_copy(src, dst, s_wkv.at[i]) for i, (src, dst) in enumerate(((wk_h, wk), (wv_h, wv)))]
    c_wo = []
    for r in range(2 * n_y):
        dest = lax.rem(ypos + r // 2, n_y)
        col = pl.multiple_of(dest * blk + (r % 2) * half, 128)
        c_wo.append(pltpu.make_async_copy(wo_h.at[:, pl.ds(col, half)], wo.at[r], s_wo.at[r]))
    n_groups = rows // GROUP

    def ring_copies(group):
        seqs = pl.ds(group * GROUP, GROUP)
        slot = group % RING
        return (pltpu.make_async_copy(sk_h.at[seqs], ring_k.at[slot], s_ring.at[slot, 0]),
                pltpu.make_async_copy(sv_h.at[seqs], ring_v.at[slot], s_ring.at[slot, 1]))

    def start(copies):
        for c in copies:
            c.start()

    def wait(copies):
        for c in copies:
            c.wait()

    c_hid.start()
    c_wq[0].start()
    start(c_raw)

    barrier = pltpu.get_barrier_semaphore()
    for where in (partner, left, right, up, down):
        pl.semaphore_signal(barrier, inc=1, device_id=where, device_id_type=MESH)

    def deinterleave(which):
        for i, dst in enumerate((kpre, vpre)):
            flat[...] = raw[which, i].astype(F32)
            for kv in range(kv_n):
                dst[kv, pl.ds(which * local_pos, local_pos), :] = flat[pl.ds(kv, local_pos, stride=kv_n), :].astype(BF16)

    def queries(kv):
        part = dot_nn(hid[...], wq[kv]).astype(BF16)
        qg[0, kv] = part
        for g in range(grp):
            q8[pl.ds(kv * grp + g, rows, stride=heads), :] = part[:, g * head:(g + 1) * head].astype(F32)

    def send_queries(kv):
        pair = (remote(qg.at[0, kv], qg.at[1, kv], s_qs.at[0, kv], s_qr.at[1, kv], right),
                remote(qg.at[0, kv], qg.at[2, kv], s_qs.at[1, kv], s_qr.at[2, kv], left))
        start(pair)
        return pair

    c_hid.wait()
    c_wq[0].wait()
    c_wq[1].start()
    start(c_wkv)
    queries(0)
    wait(c_raw)
    deinterleave(0)
    pl.semaphore_wait(barrier, 5)
    q_copies = [send_queries(0)]
    c_swap = [remote(src, raw.at[1, i], s_rawsend.at[i], s_rawrecv.at[i], partner) for i, src in enumerate((pk_h, pv_h))]
    start(c_swap)
    c_wq[1].wait()
    start(ring_copies(0))
    queries(1)
    q_copies.append(send_queries(1))
    start(ring_copies(1))
    start(c_wo)

    wait(c_wkv)
    knew[...] = dot_nn(hid[...], wk[...]).astype(BF16).astype(F32)
    vnew[...] = dot_nn(hid[...], wv[...]).astype(BF16).astype(F32)

    wait(c_swap)
    deinterleave(1)

    n_pos = kpre.shape[1]

    def prefix_pair(slot_a, slot_b, kv, chunk, buf):
        at_rows = pl.ds(chunk * part_rows, part_rows)
        stacked = jnp.concatenate([qg[slot, kv, at_rows, pl.ds(g * head, head)]
                                   for slot in (slot_a, slot_b) for g in range(grp)], axis=0)
        run = None
        for c in range(n_pos // POS_CHUNK):
            at = pl.ds(c * POS_CHUNK, POS_CHUNK)
            s = dot_nt(stacked, kpre[kv, at, :])
            scores[buf, :, at] = s
            for t in range(POS_CHUNK // 128):
                piece = s[:, t * 128:(t + 1) * 128]
                run = piece if run is None else jnp.maximum(run, piece)
        row_max = jnp.max(run, axis=1, keepdims=True) * scale
        wide_max = jnp.broadcast_to(row_max, (2 * stack, 128))
        wide_max = jnp.concatenate([wide_max] * (POS_CHUNK // 128), axis=1)
        total, num = None, None
        for c in range(n_pos // POS_CHUNK):
            at = pl.ds(c * POS_CHUNK, POS_CHUNK)
            p = jnp.exp2(scores[buf, :, at] * scale - wide_max)
            for t in range(POS_CHUNK // 128):
                piece = p[:, t * 128:(t + 1) * 128]
                total = piece if total is None else total + piece
            term = dot_nn(p.astype(BF16), vpre[kv, at, :])
            num = term if num is None else num + term
        row_sum = jnp.sum(total, axis=1, keepdims=True)
        return ((num[:stack], row_max[:stack], row_sum[:stack]), (num[stack:], row_max[stack:], row_sum[stack:]))

    sent = []

    def x_copies(i, where):
        return (remote(xs_num.at[i], xr_num.at[i], s_xs.at[i], s_xr.at[i], where),
                remote(xs_st.at[i], xr_st.at[i], s_xst.at[i], s_xrt.at[i], where))

    def post(state, i, where):
        xs_num[i] = state[0]
        xs_st[i] = pack_stats(state[1], state[2])
        out = x_copies(i, where)
        start(out)
        sent.extend(out)

    def received(i, where):
        for c in x_copies(i, where):
            c.wait_recv()
        return (xr_num[i],) + unpack_stats(xr_st[i])

    def keep(refs, i, state):
        refs[0][i] = state[0]
        lane = lax.broadcasted_iota(jnp.int32, state[0].shape, 1)
        refs[1][i] = jnp.where(lane == 0, state[1], state[2])

    def kept(refs, i):
        return refs[0][i], refs[1][i][:, 0:1], refs[1][i][:, 1:2]

    own = (own_num, own_st)
    hold = (hold_num, hold_st)

    def prefix_near(chunk):
        base = 6 * chunk
        on_right, on_left = prefix_pair(2, 1, 1, chunk, 0)
        post(on_right, base, right)
        keep(hold, 1, on_left)
        on_right, on_left = prefix_pair(2, 1, 0, chunk, 1)
        post(on_left, base + 1, left)
        keep(hold, 0, on_right)

    def prefix_far(chunk):
        base = 6 * chunk
        across, mine = prefix_pair(3, 0, 0, chunk, 0)
        post(across, base + 2, right)
        keep(own, 0, mine)
        across, mine = prefix_pair(3, 0, 1, chunk, 1)
        post(across, base + 3, left)
        keep(own, 1, mine)

    def relay(chunk):
        base = 6 * chunk
        post(merge(received(base + 2, right), kept(hold, 0)), base + 4, right)
        post(merge(received(base + 3, left), kept(hold, 1)), base + 5, left)

    lines = GROUP * heads
    span = ring_k.shape[2]
    tile = span // 4

    def suffix_group(group):
        slot = group % RING
        lane = lax.broadcasted_iota(jnp.int32, (head, lines), 1)
        q_t = jnp.transpose(q8[pl.ds(group * lines, lines), :])
        for j in range(GROUP // 2):
            both = [jnp.where(lane // heads == 2 * j + e, q_t, 0.0) for e in range(2)]
            qbd[j] = jnp.concatenate(both, axis=0).astype(BF16)
        one = lax.broadcasted_iota(jnp.int32, (1, lines), 1)
        length = jnp.zeros((1, lines), jnp.int32)
        for b in range(GROUP):
            length = jnp.where(one // heads == b, lens[group * GROUP + b], length)
        line = lax.broadcasted_iota(jnp.int32, (tile, lines), 0)
        lane = lax.broadcasted_iota(jnp.int32, (tile, lines), 1)
        mine = lax.rem(line, kv_n) == lax.rem(lane, heads) // grp
        place = jnp.where(mine, line // kv_n, span)
        wait(ring_copies(group))
        run = jnp.full((1, lines), LOW, F32)
        for c in range(4):
            at = pl.ds(c * tile, tile)
            s = None
            for j in range(GROUP // 2):
                keys = jnp.concatenate([ring_k[slot, 2 * j, at, :], ring_k[slot, 2 * j + 1, at, :]], axis=1)
                term = dot_nn(keys, qbd[j])
                s = term if s is None else s + term
            s = jnp.where(place < length - c * (tile // kv_n), s * scale, -jnp.inf)
            sufs[at, :] = s
            run = jnp.maximum(run, jnp.max(s, axis=0, keepdims=True))
        total = jnp.zeros((1, lines), F32)
        for c in range(4):
            p = jnp.exp2(sufs[pl.ds(c * tile, tile), :] - run)
            total = total + jnp.sum(p, axis=0, keepdims=True)
            sufp[:, pl.ds(c * tile, tile)] = jnp.transpose(p).astype(BF16)
        stats = jnp.concatenate([run, total, jnp.zeros((head - 2, lines), F32)], axis=0)
        sst8[pl.ds(group * lines, lines), :] = jnp.transpose(stats)
        for j in range(GROUP // 2):
            weights = sufp[pl.ds(2 * j * heads, 2 * heads), :]
            for e in range(2):
                o = dot_nn(weights, ring_v[slot, 2 * j + e])
                so8[pl.ds(group * lines + (2 * j + e) * heads, heads), :] = o[e * heads:(e + 1) * heads]
        if group + RING < n_groups:
            start(ring_copies(group + RING))

    def combine(chunk):
        base = 6 * chunk
        for kv in range(kv_n):
            states = [kept(own, kv)]
            if kv == 0:
                states += [received(base + 1, left), received(base + 4, right)]
            else:
                states += [received(base, right), received(base + 5, left)]
            state = functools.reduce(merge, states)
            rest = []
            for g in range(grp):
                every = pl.ds(chunk * part_rows * heads + kv * grp + g, part_rows, stride=heads)
                stats = sst8[every, :]
                rest.append((so8[every, :], stats[:, 0:1], stats[:, 1:2], q8[every, :]))
            num, top, tot, qs = (jnp.concatenate(list(v), axis=0) for v in zip(*rest))
            state = merge(state, (num, top, tot))
            at_rows = pl.ds(chunk * part_rows, part_rows)
            kn = jnp.concatenate([knew[at_rows, pl.ds(kv * head, head)]] * grp, axis=0)
            vn = jnp.concatenate([vnew[at_rows, pl.ds(kv * head, head)]] * grp, axis=0)
            s_new = jnp.sum(qs * kn, axis=1, keepdims=True) * scale
            state = merge(state, (vn, s_new, jnp.ones_like(s_new)))
            res = (state[0] / state[2]).astype(BF16)
            for g in range(grp):
                att[chunk, :, pl.ds((kv * grp + g) * head, head)] = res[g * part_rows:(g + 1) * part_rows]

    ysent = []

    def y_part(chunk, r):
        if chunk == 0:
            c_wo[r].wait()
        return dot_nn(att[chunk], wo[r])

    def y_copy(i, where):
        return remote(ys.at[i], yr.at[i], s_ys.at[i], s_yr.at[i], where)

    def y_post(val, i, where):
        ys[i] = val
        c = y_copy(i, where)
        c.start()
        ysent.append(c)

    far, near_up, near_down = 2 * (n_y // 2), 2, 2 * (n_y - 1)

    def project(chunk):
        base = 6 * chunk
        y_post(y_part(chunk, far), base, up)
        y_post(y_part(chunk, far + 1), base + 1, down)
        y_post(y_part(chunk, near_up + 1), base + 2, up)
        y_post(y_part(chunk, near_down), base + 3, down)
        yhold[0] = y_part(chunk, near_up)
        yhold[1] = y_part(chunk, near_down + 1)
        yhold[2] = y_part(chunk, 0)
        yhold[3] = y_part(chunk, 1)

    def y_relay(chunk):
        base = 6 * chunk
        y_copy(base, up).wait_recv()
        y_post(yhold[0] + yr[base], base + 4, up)
        y_copy(base + 1, down).wait_recv()
        y_post(yhold[1] + yr[base + 1], base + 5, down)

    gsend = []

    def g_copy(src, chunk, slot, part, sem, where):
        return remote(src, ygat.at[chunk, slot, part], s_gs.at[chunk, sem], s_gr.at[chunk, slot, part], where)

    outs = []

    def put(src, chunk, dest, part):
        col = pl.multiple_of(dest * blk + part * half, 128)
        c = pltpu.make_async_copy(src, out_h.at[pl.ds(chunk * part_rows, part_rows), pl.ds(col, half)], s_out.at[len(outs)])
        c.start()
        outs.append(c)

    def g_out(chunk, slot, part, where, sem):
        src = yblk.at[chunk, part] if slot < 2 else ygat.at[chunk, 0 if part == 0 else 1, part]
        return g_copy(src, chunk, slot, part, sem, where)

    def finish(chunk):
        base = 6 * chunk
        at_rows = pl.ds(chunk * part_rows, part_rows)
        for part, (near, merged) in enumerate(((base + 3, base + 4), (base + 2, base + 5))):
            val = yhold[2 + part]
            for i in (near, merged):
                y_copy(i, up if i % 2 == 0 else down).wait_recv()
                val = val + yr[i]
            col = pl.multiple_of(ypos * blk + part * half, 128)
            yblk[chunk, part] = (val + hid[at_rows, pl.ds(col, half)].astype(F32)).astype(BF16)
            first, second = ((0, up, part), (1, down, 2 + part)) if part == 0 else ((1, down, 2 + part), (0, up, part))
            for slot, where, sem in (first, second):
                c = g_out(chunk, slot, part, where, sem)
                c.start()
                gsend.append(c)
            put(yblk.at[chunk, part], chunk, ypos, part)

    def forward(chunk):
        g_out(chunk, 0, 0, up, 0).wait_recv()
        c = g_out(chunk, 2, 0, up, 4)
        c.start()
        gsend.append(c)
        g_out(chunk, 1, 1, down, 3).wait_recv()
        c = g_out(chunk, 2, 1, down, 5)
        c.start()
        gsend.append(c)
        put(ygat.at[chunk, 0, 0], chunk, below, 0)
        put(ygat.at[chunk, 1, 1], chunk, above, 1)

    def collect(chunk):
        g_out(chunk, 0, 1, up, 1).wait_recv()
        put(ygat.at[chunk, 0, 1], chunk, below, 1)
        g_out(chunk, 1, 0, down, 2).wait_recv()
        put(ygat.at[chunk, 1, 0], chunk, above, 0)
        g_out(chunk, 2, 0, up, 4).wait_recv()
        put(ygat.at[chunk, 2, 0], chunk, opposite, 0)
        g_out(chunk, 2, 1, down, 5).wait_recv()
        put(ygat.at[chunk, 2, 1], chunk, opposite, 1)

    q_copies[0][0].wait_recv()
    fwd_right = remote(qg.at[1, 0], qg.at[3, 0], s_qs.at[2, 0], s_qr.at[3, 0], right)
    fwd_right.start()
    q_copies[1][1].wait_recv()
    fwd_left = remote(qg.at[2, 1], qg.at[3, 1], s_qs.at[2, 1], s_qr.at[3, 1], left)
    fwd_left.start()
    q_copies[1][0].wait_recv()
    q_copies[0][1].wait_recv()

    per_part = n_groups // 2
    prefix_near(0)
    fwd_right.wait_recv()
    fwd_left.wait_recv()
    prefix_far(0)
    for group in range(per_part // 2):
        suffix_group(group)
    relay(0)
    for group in range(per_part // 2, per_part):
        suffix_group(group)
    combine(0)
    project(0)

    prefix_near(1)
    y_relay(0)
    prefix_far(1)
    for group in range(per_part, per_part + per_part // 2):
        suffix_group(group)
    finish(0)
    relay(1)
    for group in range(per_part + per_part // 2, n_groups):
        suffix_group(group)
    forward(0)
    combine(1)
    project(1)
    collect(0)
    y_relay(1)
    finish(1)
    forward(1)
    collect(1)

    for pair in q_copies:
        for c in pair:
            c.wait_send()
    for c in [fwd_right, fwd_left] + sent + ysent + gsend:
        c.wait_send()
    wait(outs)


def solution(mesh):
    n_ctx, n_y = mesh.shape['ctx'], mesh.shape['heads']
    row_spec = P(('dp', 'ctx'), None)
    col_spec = P(None, 'heads')
    pre_spec = P(('dp', 'ctx'), 'heads', None)
    suf_spec = P(('dp', 'ctx'), None, 'heads', None)

    def local_step(hidden, w_query, w_key, w_value, w_out, prefix_k, prefix_v, suffix_k, suffix_v, seq_lens):
        rows, width = hidden.shape
        pos, kv_n, head = prefix_k.shape
        slots = suffix_k.shape[1]
        grp = w_query.shape[1] // (kv_n * head)
        heads = kv_n * grp
        blk = width // n_y
        half_rows = rows // 2
        stack = grp * half_rows
        lines = GROUP * heads
        dma = pltpu.SemaphoreType.DMA
        scratch = dict(
            hid=pltpu.VMEM((rows, width), BF16),
            wq=pltpu.VMEM((kv_n, width, grp * head), BF16),
            wk=pltpu.VMEM((width, kv_n * head), BF16),
            wv=pltpu.VMEM((width, kv_n * head), BF16),
            wo=pltpu.VMEM((2 * n_y, heads * head, blk // 2), BF16),
            raw=pltpu.VMEM((2, 2, pos * kv_n, head), BF16),
            flat=pltpu.VMEM((pos * kv_n, head), F32),
            kpre=pltpu.VMEM((kv_n, 2 * pos, head), BF16),
            vpre=pltpu.VMEM((kv_n, 2 * pos, head), BF16),
            qg=pltpu.VMEM((4, kv_n, rows, grp * head), BF16),
            q8=pltpu.VMEM((rows * heads, head), F32),
            knew=pltpu.VMEM((rows, kv_n * head), F32),
            vnew=pltpu.VMEM((rows, kv_n * head), F32),
            ring_k=pltpu.VMEM((RING, GROUP, slots * kv_n, head), BF16),
            ring_v=pltpu.VMEM((RING, GROUP, slots * kv_n, head), BF16),
            qbd=pltpu.VMEM((GROUP // 2, 2 * head, lines), BF16),
            sufs=pltpu.VMEM((slots * kv_n, lines), F32),
            sufp=pltpu.VMEM((lines, slots * kv_n), BF16),
            scores=pltpu.VMEM((2, 2 * stack, 2 * pos), F32),
            own_num=pltpu.VMEM((kv_n, stack, head), F32),
            own_st=pltpu.VMEM((kv_n, stack, 128), F32),
            hold_num=pltpu.VMEM((2, stack, head), F32),
            hold_st=pltpu.VMEM((2, stack, 128), F32),
            so8=pltpu.VMEM((rows * heads, head), F32),
            sst8=pltpu.VMEM((rows * heads, head), F32),
            xs_num=pltpu.VMEM((12, stack, head), F32),
            xs_st=pltpu.VMEM((12, 8, stack), F32),
            xr_num=pltpu.VMEM((12, stack, head), F32),
            xr_st=pltpu.VMEM((12, 8, stack), F32),
            att=pltpu.VMEM((2, half_rows, heads * head), BF16),
            yhold=pltpu.VMEM((4, half_rows, blk // 2), F32),
            ys=pltpu.VMEM((12, half_rows, blk // 2), F32),
            yr=pltpu.VMEM((12, half_rows, blk // 2), F32),
            yblk=pltpu.VMEM((2, 2, half_rows, blk // 2), BF16),
            ygat=pltpu.VMEM((2, 3, 2, half_rows, blk // 2), BF16),
            s_hid=dma(()), s_wq=dma((kv_n,)), s_wkv=dma((2,)), s_wo=dma((2 * n_y,)),
            s_raw=dma((2,)), s_rawsend=dma((2,)), s_rawrecv=dma((2,)), s_ring=dma((RING, 2)),
            s_qs=dma((3, kv_n)), s_qr=dma((4, kv_n)),
            s_xs=dma((12,)), s_xr=dma((12,)), s_xst=dma((12,)), s_xrt=dma((12,)),
            s_ys=dma((12,)), s_yr=dma((12,)), s_gs=dma((2, 6)), s_gr=dma((2, 3, 2)), s_out=dma((16,)),
        )
        hbm = pl.BlockSpec(memory_space=pl.ANY)
        return pl.pallas_call(
            functools.partial(kernel, (n_ctx, n_y, kv_n, grp)),
            out_shape=jax.ShapeDtypeStruct((rows, width), BF16),
            in_specs=[hbm] * 9 + [pl.BlockSpec(memory_space=pltpu.SMEM)],
            out_specs=hbm,
            scratch_shapes=list(scratch.values()),
            compiler_params=pltpu.CompilerParams(collective_id=0, has_side_effects=True, vmem_limit_bytes=67043328),
        )(hidden, w_query, w_key, w_value, w_out,
          prefix_k.reshape(pos * kv_n, head), prefix_v.reshape(pos * kv_n, head),
          suffix_k.reshape(rows, slots * kv_n, head), suffix_v.reshape(rows, slots * kv_n, head), seq_lens)

    return jax.shard_map(local_step, mesh=mesh, in_specs=(row_spec, col_spec, col_spec, col_spec, P('heads', None), pre_spec, pre_spec, suf_spec, suf_spec, P(('dp', 'ctx'))), out_specs=row_spec, check_vma=False)
```

time: 182 us -> 61.8 us (0.34)
  the two profiles are of different devices: /device:TPU:97 before, /device:TPU:106 now
where the time goes in v2:
time: 61.8 us; the launch traced here: 61.7 us
  Pallas kernels  59.7 us (97%)
  local copies, waits for them, and re-layouts  1.97 us (3%)
    pallas_call x1, Pallas kernels, local_step(): pl.pallas_call(functools.partial(kernel, (n_ctx, n_y, kv_n, grp)), out_sh...  59.7 us
    unnamed x1, local copies, waits for them, and re-layouts  1.97 us

profile of v2, /device:TPU:106, one launch (start us, length us, event | category | flops | bytes accessed | tf_op | source)
XLA Modules:
  0.0 61.7 jit_solution(13520074228648936098)
XLA Ops:
  0.0 59.7 %shard_map.100 = bf16[64,5120]{1,0:T(8,128)(2,1)} custom-call(bf16[64,5120]{1,0:T(8,128)(2,1)} %hid_h.1, bf16[5120,1024]{1,0:T(8,128)(2,1)} %wq_h.1, bf16[5120,256]{1,0:T(8,128)(2,1)} %wk_h.1, bf16[5120,256]{1,0:T(8,128)(2,1)} %wv_h.1, bf16[1024,5120]{1,0:T(8,128)(2,1)} %wo_h.1, bf16[2048,128]{1,0:T(8,128)(2,1)} %bitcast.6, bf16[2048,128]{1,0:T(8,128)(2,1)} %bitcast.7, ...), custom_call_target="tpu_custom_call" | custom-call | tf_op jit(solution)/shard_map/pallas_call | solution.py:507
  59.7 2.0 %copy.12 = bf16[64,5120]{1,0:T(8,128)(2,1)} copy(bf16[64,5120]{1,0:T(8,128)(2,1)} %shard_map.100) | data formatting | bytes 1310720

commit v3 on v2

--- a/solution.py
+++ b/solution.py
@@ -14,6 +14,8 @@
 GROUP = 16
 RING = 2
 POS_CHUNK = 512
+PIECES = 4
+VMEM_BYTES = 66000000
 
 
 def dot_nt(a, b):
@@ -44,12 +46,12 @@
     return num_a * fac_a + num_b * fac_b, top, sum_a * fac_a + sum_b * fac_b
 
 
-def kernel(dims, hid_h, wq_h, wk_h, wv_h, wo_h, pk_h, pv_h, sk_h, sv_h, lens, out_h,
+def kernel(dims, hid_h, wq_h, wk_h, wv_h, wo_h, pk_h, pv_h, sk_h, sv_h, lens, out_v,
            hid, wq, wk, wv, wo, raw, flat, kpre, vpre, qg, q8, knew, vnew,
            ring_k, ring_v, qbd, sufs, sufp, scores, own_num, own_st, hold_num, hold_st,
-           so8, sst8, xs_num, xs_st, xr_num, xr_st, att, yhold, ys, yr, yblk, ygat,
+           so8, sst8, xs_num, xs_st, xr_num, xr_st, att, yhold, ys, yr,
            s_hid, s_wq, s_wkv, s_wo, s_raw, s_rawsend, s_rawrecv, s_ring,
-           s_qs, s_qr, s_xs, s_xr, s_xst, s_xrt, s_ys, s_yr, s_gs, s_gr, s_out):
+           s_qs, s_qr, s_xs, s_xr, s_xst, s_xrt, s_ys, s_yr, s_gs, s_gr):
     n_ctx, n_y, kv_n, grp = dims
     rows = hid.shape[0]
     width = hid.shape[1]
@@ -69,7 +71,7 @@
     partner = {'ctx': ctx + 1 - 2 * lax.rem(ctx, 2)}
     up = {'heads': lax.rem(ypos + 1, n_y)}
     down = {'heads': lax.rem(ypos + n_y - 1, n_y)}
-    below, above, opposite = lax.rem(ypos + n_y - 1, n_y), lax.rem(ypos + 1, n_y), lax.rem(ypos + n_y // 2, n_y)
+    below, above = lax.rem(ypos + n_y - 1, n_y), lax.rem(ypos + 1, n_y)
 
     def remote(src, dst, send, recv, where):
         return pltpu.make_async_remote_copy(src_ref=src, dst_ref=dst, send_sem=send, recv_sem=recv,
@@ -77,7 +79,10 @@
 
     c_hid = pltpu.make_async_copy(hid_h, hid, s_hid)
     c_raw = [pltpu.make_async_copy(src, raw.at[0, i], s_raw.at[i]) for i, src in enumerate((pk_h, pv_h))]
-    c_wq = [pltpu.make_async_copy(wq_h.at[:, pl.ds(kv * grp * head, grp * head)], wq.at[kv], s_wq.at[kv]) for kv in range(kv_n)]
+    deep = width // PIECES
+    c_wq = [pltpu.make_async_copy(wq_h.at[pl.ds(k * deep, deep), pl.ds(kv * grp * head, grp * head)],
+                                  wq.at[kv, pl.ds(k * deep, deep), :], s_wq.at[kv, k])
+            for kv in range(kv_n) for k in range(PIECES)]
     c_wkv = [pltpu.make_async_copy(src, dst, s_wkv.at[i]) for i, (src, dst) in enumerate(((wk_h, wk), (wv_h, wv)))]
     c_wo = []
     for r in range(2 * n_y):
@@ -100,9 +105,15 @@
         for c in copies:
             c.wait()
 
+    queue = c_wq + c_raw + c_wkv
+
+    def advance():
+        if queue:
+            queue.pop(0).start()
+
     c_hid.start()
-    c_wq[0].start()
-    start(c_raw)
+    for _ in range(3):
+        advance()
 
     barrier = pltpu.get_barrier_semaphore()
     for where in (partner, left, right, up, down):
@@ -115,7 +126,14 @@
                 dst[kv, pl.ds(which * local_pos, local_pos), :] = flat[pl.ds(kv, local_pos, stride=kv_n), :].astype(BF16)
 
     def queries(kv):
-        part = dot_nn(hid[...], wq[kv]).astype(BF16)
+        total = None
+        for k in range(PIECES):
+            c_wq[kv * PIECES + k].wait()
+            advance()
+            at = pl.ds(k * deep, deep)
+            term = dot_nn(hid[:, at], wq[kv, at, :])
+            total = term if total is None else total + term
+        part = total.astype(BF16)
         qg[0, kv] = part
         for g in range(grp):
             q8[pl.ds(kv * grp + g, rows, stride=heads), :] = part[:, g * head:(g + 1) * head].astype(F32)
@@ -127,58 +145,69 @@
         return pair
 
     c_hid.wait()
-    c_wq[0].wait()
-    c_wq[1].start()
-    start(c_wkv)
     queries(0)
-    wait(c_raw)
-    deinterleave(0)
     pl.semaphore_wait(barrier, 5)
     q_copies = [send_queries(0)]
     c_swap = [remote(src, raw.at[1, i], s_rawsend.at[i], s_rawrecv.at[i], partner) for i, src in enumerate((pk_h, pv_h))]
     start(c_swap)
-    c_wq[1].wait()
-    start(ring_copies(0))
     queries(1)
     q_copies.append(send_queries(1))
-    start(ring_copies(1))
-    start(c_wo)
+    while queue:
+        advance()
+    wait(c_raw)
+    deinterleave(0)
 
     wait(c_wkv)
+    start(ring_copies(0))
     knew[...] = dot_nn(hid[...], wk[...]).astype(BF16).astype(F32)
     vnew[...] = dot_nn(hid[...], wv[...]).astype(BF16).astype(F32)
 
     wait(c_swap)
     deinterleave(1)
+    start(ring_copies(1))
+    for r in (4, 5, 3, 6, 2, 7, 0, 1):
+        c_wo[r].start()
 
     n_pos = kpre.shape[1]
 
-    def prefix_pair(slot_a, slot_b, kv, chunk, buf):
-        at_rows = pl.ds(chunk * part_rows, part_rows)
-        stacked = jnp.concatenate([qg[slot, kv, at_rows, pl.ds(g * head, head)]
-                                   for slot in (slot_a, slot_b) for g in range(grp)], axis=0)
-        run = None
-        for c in range(n_pos // POS_CHUNK):
+    n_pieces = n_pos // POS_CHUNK
+    part_lanes = POS_CHUNK // 128
+
+    def prefix_states(jobs):
+        stacked, run, out = [None] * len(jobs), [None] * len(jobs), []
+
+        def score(i, c):
+            sources, kv = jobs[i]
+            if c == 0:
+                stacked[i] = jnp.concatenate([qg[slot, kv, pl.ds(chunk * part_rows, part_rows), pl.ds(g * head, head)]
+                                              for slot, chunk in sources for g in range(grp)], axis=0)
             at = pl.ds(c * POS_CHUNK, POS_CHUNK)
-            s = dot_nt(stacked, kpre[kv, at, :])
-            scores[buf, :, at] = s
-            for t in range(POS_CHUNK // 128):
+            s = dot_nt(stacked[i], kpre[kv, at, :])
+            scores[i % 2, :, at] = s
+            for t in range(part_lanes):
                 piece = s[:, t * 128:(t + 1) * 128]
-                run = piece if run is None else jnp.maximum(run, piece)
-        row_max = jnp.max(run, axis=1, keepdims=True) * scale
-        wide_max = jnp.broadcast_to(row_max, (2 * stack, 128))
-        wide_max = jnp.concatenate([wide_max] * (POS_CHUNK // 128), axis=1)
-        total, num = None, None
-        for c in range(n_pos // POS_CHUNK):
-            at = pl.ds(c * POS_CHUNK, POS_CHUNK)
-            p = jnp.exp2(scores[buf, :, at] * scale - wide_max)
-            for t in range(POS_CHUNK // 128):
-                piece = p[:, t * 128:(t + 1) * 128]
-                total = piece if total is None else total + piece
-            term = dot_nn(p.astype(BF16), vpre[kv, at, :])
-            num = term if num is None else num + term
-        row_sum = jnp.sum(total, axis=1, keepdims=True)
-        return ((num[:stack], row_max[:stack], row_sum[:stack]), (num[stack:], row_max[stack:], row_sum[stack:]))
+                run[i] = piece if run[i] is None else jnp.maximum(run[i], piece)
+
+        for c in range(n_pieces):
+            score(0, c)
+        for i, (sources, kv) in enumerate(jobs):
+            row_max = jnp.max(run[i], axis=1, keepdims=True) * scale
+            wide_max = jnp.broadcast_to(row_max, (2 * stack, 128))
+            wide_max = jnp.concatenate([wide_max] * part_lanes, axis=1)
+            total, num = None, None
+            for c in range(n_pieces):
+                if i + 1 < len(jobs):
+                    score(i + 1, c)
+                at = pl.ds(c * POS_CHUNK, POS_CHUNK)
+                p = jnp.exp2(scores[i % 2, :, at] * scale - wide_max)
+                for t in range(part_lanes):
+                    piece = p[:, t * 128:(t + 1) * 128]
+                    total = piece if total is None else total + piece
+                term = dot_nn(p.astype(BF16), vpre[kv, at, :])
+                num = term if num is None else num + term
+            row_sum = jnp.sum(total, axis=1, keepdims=True)
+            out += [(num[:stack], row_max[:stack], row_sum[:stack]), (num[stack:], row_max[stack:], row_sum[stack:])]
+        return out
 
     sent = []
 
@@ -211,21 +240,24 @@
 
     def prefix_near(chunk):
         base = 6 * chunk
-        on_right, on_left = prefix_pair(2, 1, 1, chunk, 0)
-        post(on_right, base, right)
-        keep(hold, 1, on_left)
-        on_right, on_left = prefix_pair(2, 1, 0, chunk, 1)
-        post(on_left, base + 1, left)
-        keep(hold, 0, on_right)
-
-    def prefix_far(chunk):
-        base = 6 * chunk
-        across, mine = prefix_pair(3, 0, 0, chunk, 0)
-        post(across, base + 2, right)
-        keep(own, 0, mine)
-        across, mine = prefix_pair(3, 0, 1, chunk, 1)
-        post(across, base + 3, left)
-        keep(own, 1, mine)
+        both = ((2, chunk), (1, chunk))
+        right_1, left_1, right_0, left_0 = prefix_states([(both, 1), (both, 0)])
+        post(right_1, base, right)
+        post(left_0, base + 1, left)
+        keep(hold, 1, left_1)
+        keep(hold, 0, right_0)
+
+    def prefix_far():
+        both = ((3, 0), (3, 1))
+        states = prefix_states([(both, 0), (both, 1)])
+        for chunk in range(2):
+            post(states[chunk], 6 * chunk + 2, right)
+            post(states[2 + chunk], 6 * chunk + 3, left)
+
+    def prefix_own():
+        both = ((0, 0), (0, 1))
+        for i, state in enumerate(prefix_states([(both, 0), (both, 1)])):
+            keep(own, i, state)
 
     def relay(chunk):
         base = 6 * chunk
@@ -281,7 +313,7 @@
     def combine(chunk):
         base = 6 * chunk
         for kv in range(kv_n):
-            states = [kept(own, kv)]
+            states = [kept(own, 2 * kv + chunk)]
             if kv == 0:
                 states += [received(base + 1, left), received(base + 4, right)]
             else:
@@ -341,20 +373,10 @@
 
     gsend = []
 
-    def g_copy(src, chunk, slot, part, sem, where):
-        return remote(src, ygat.at[chunk, slot, part], s_gs.at[chunk, sem], s_gr.at[chunk, slot, part], where)
-
-    outs = []
-
-    def put(src, chunk, dest, part):
-        col = pl.multiple_of(dest * blk + part * half, 128)
-        c = pltpu.make_async_copy(src, out_h.at[pl.ds(chunk * part_rows, part_rows), pl.ds(col, half)], s_out.at[len(outs)])
-        c.start()
-        outs.append(c)
-
     def g_out(chunk, slot, part, where, sem):
-        src = yblk.at[chunk, part] if slot < 2 else ygat.at[chunk, 0 if part == 0 else 1, part]
-        return g_copy(src, chunk, slot, part, sem, where)
+        dest = ypos if slot < 2 else (below if part == 0 else above)
+        at = (pl.ds(chunk * part_rows, part_rows), pl.ds(pl.multiple_of(dest * blk + part * half, 128), half))
+        return remote(out_v.at[at], out_v.at[at], s_gs.at[chunk, sem], s_gr.at[chunk, slot, part], where)
 
     def finish(chunk):
         base = 6 * chunk
@@ -365,13 +387,12 @@
                 y_copy(i, up if i % 2 == 0 else down).wait_recv()
                 val = val + yr[i]
             col = pl.multiple_of(ypos * blk + part * half, 128)
-            yblk[chunk, part] = (val + hid[at_rows, pl.ds(col, half)].astype(F32)).astype(BF16)
+            out_v[at_rows, pl.ds(col, half)] = (val + hid[at_rows, pl.ds(col, half)].astype(F32)).astype(BF16)
             first, second = ((0, up, part), (1, down, 2 + part)) if part == 0 else ((1, down, 2 + part), (0, up, part))
             for slot, where, sem in (first, second):
                 c = g_out(chunk, slot, part, where, sem)
                 c.start()
                 gsend.append(c)
-            put(yblk.at[chunk, part], chunk, ypos, part)
 
     def forward(chunk):
         g_out(chunk, 0, 0, up, 0).wait_recv()
@@ -382,19 +403,14 @@
         c = g_out(chunk, 2, 1, down, 5)
         c.start()
         gsend.append(c)
-        put(ygat.at[chunk, 0, 0], chunk, below, 0)
-        put(ygat.at[chunk, 1, 1], chunk, above, 1)
 
     def collect(chunk):
         g_out(chunk, 0, 1, up, 1).wait_recv()
-        put(ygat.at[chunk, 0, 1], chunk, below, 1)
         g_out(chunk, 1, 0, down, 2).wait_recv()
-        put(ygat.at[chunk, 1, 0], chunk, above, 0)
         g_out(chunk, 2, 0, up, 4).wait_recv()
-        put(ygat.at[chunk, 2, 0], chunk, opposite, 0)
         g_out(chunk, 2, 1, down, 5).wait_recv()
-        put(ygat.at[chunk, 2, 1], chunk, opposite, 1)
-
+
+    prefix_own()
     q_copies[0][0].wait_recv()
     fwd_right = remote(qg.at[1, 0], qg.at[3, 0], s_qs.at[2, 0], s_qr.at[3, 0], right)
     fwd_right.start()
@@ -408,27 +424,23 @@
     prefix_near(0)
     fwd_right.wait_recv()
     fwd_left.wait_recv()
-    prefix_far(0)
-    for group in range(per_part // 2):
+    prefix_far()
+    for group in range(per_part):
         suffix_group(group)
     relay(0)
-    for group in range(per_part // 2, per_part):
-        suffix_group(group)
+    prefix_near(1)
     combine(0)
     project(0)
 
-    prefix_near(1)
+    suffix_group(per_part)
     y_relay(0)
-    prefix_far(1)
-    for group in range(per_part, per_part + per_part // 2):
+    relay(1)
+    for group in range(per_part + 1, n_groups):
         suffix_group(group)
     finish(0)
-    relay(1)
-    for group in range(per_part + per_part // 2, n_groups):
-        suffix_group(group)
-    forward(0)
     combine(1)
     project(1)
+    forward(0)
     collect(0)
     y_relay(1)
     finish(1)
@@ -440,7 +452,12 @@
             c.wait_send()
     for c in [fwd_right, fwd_left] + sent + ysent + gsend:
         c.wait_send()
-    wait(outs)
+
+
+def store(src, dst, sem):
+    c = pltpu.make_async_copy(src, dst, sem)
+    c.start()
+    c.wait()
 
 
 def solution(mesh):
@@ -481,8 +498,8 @@
             sufs=pltpu.VMEM((slots * kv_n, lines), F32),
             sufp=pltpu.VMEM((lines, slots * kv_n), BF16),
             scores=pltpu.VMEM((2, 2 * stack, 2 * pos), F32),
-            own_num=pltpu.VMEM((kv_n, stack, head), F32),
-            own_st=pltpu.VMEM((kv_n, stack, 128), F32),
+            own_num=pltpu.VMEM((2 * kv_n, stack, head), F32),
+            own_st=pltpu.VMEM((2 * kv_n, stack, 128), F32),
             hold_num=pltpu.VMEM((2, stack, head), F32),
             hold_st=pltpu.VMEM((2, stack, 128), F32),
             so8=pltpu.VMEM((rows * heads, head), F32),
@@ -495,24 +512,30 @@
             yhold=pltpu.VMEM((4, half_rows, blk // 2), F32),
             ys=pltpu.VMEM((12, half_rows, blk // 2), F32),
             yr=pltpu.VMEM((12, half_rows, blk // 2), F32),
-            yblk=pltpu.VMEM((2, 2, half_rows, blk // 2), BF16),
-            ygat=pltpu.VMEM((2, 3, 2, half_rows, blk // 2), BF16),
-            s_hid=dma(()), s_wq=dma((kv_n,)), s_wkv=dma((2,)), s_wo=dma((2 * n_y,)),
+            s_hid=dma(()), s_wq=dma((kv_n, PIECES)), s_wkv=dma((2,)), s_wo=dma((2 * n_y,)),
             s_raw=dma((2,)), s_rawsend=dma((2,)), s_rawrecv=dma((2,)), s_ring=dma((RING, 2)),
             s_qs=dma((3, kv_n)), s_qr=dma((4, kv_n)),
             s_xs=dma((12,)), s_xr=dma((12,)), s_xst=dma((12,)), s_xrt=dma((12,)),
-            s_ys=dma((12,)), s_yr=dma((12,)), s_gs=dma((2, 6)), s_gr=dma((2, 3, 2)), s_out=dma((16,)),
+            s_ys=dma((12,)), s_yr=dma((12,)), s_gs=dma((2, 6)), s_gr=dma((2, 3, 2)),
         )
         hbm = pl.BlockSpec(memory_space=pl.ANY)
-        return pl.pallas_call(
+        out = pl.pallas_call(
             functools.partial(kernel, (n_ctx, n_y, kv_n, grp)),
-            out_shape=jax.ShapeDtypeStruct((rows, width), BF16),
+            out_shape=pltpu.VMEM((rows, width), BF16),
             in_specs=[hbm] * 9 + [pl.BlockSpec(memory_space=pltpu.SMEM)],
-            out_specs=hbm,
+            out_specs=pl.BlockSpec(memory_space=pltpu.VMEM),
             scratch_shapes=list(scratch.values()),
-            compiler_params=pltpu.CompilerParams(collective_id=0, has_side_effects=True, vmem_limit_bytes=67043328),
+            compiler_params=pltpu.CompilerParams(collective_id=0, has_side_effects=True, vmem_limit_bytes=VMEM_BYTES),
         )(hidden, w_query, w_key, w_value, w_out,
           prefix_k.reshape(pos * kv_n, head), prefix_v.reshape(pos * kv_n, head),
           suffix_k.reshape(rows, slots * kv_n, head), suffix_v.reshape(rows, slots * kv_n, head), seq_lens)
+        return pl.pallas_call(
+            store,
+            out_shape=jax.ShapeDtypeStruct((rows, width), BF16),
+            in_specs=[pl.BlockSpec(memory_space=pltpu.VMEM)],
+            out_specs=hbm,
+            scratch_shapes=[dma(())],
+            compiler_params=pltpu.CompilerParams(vmem_limit_bytes=1048576),
+        )(out)
 
     return jax.shard_map(local_step, mesh=mesh, in_specs=(row_spec, col_spec, col_spec, col_spec, P('heads', None), pre_spec, pre_spec, suf_spec, suf_spec, P(('dp', 'ctx'))), out_specs=row_spec, check_vma=False)

time: 61.8 us -> 61.5 us (level)
  the two profiles are of different devices: /device:TPU:106 before, /device:TPU:98 now
where the time goes in v3:
time: 61.5 us; the launch traced here: 61.4 us
  Pallas kernels  61.2 us (100%)
    pallas_call x1, Pallas kernels, local_step(): pl.pallas_call(functools.partial(kernel, (n_ctx, n_y, kv_n, grp)), out_sh...  60.4 us

profile of v3, /device:TPU:98, one launch (start us, length us, event | category | flops | bytes accessed | tf_op | source)
XLA Modules:
  0.0 61.4 jit_solution(8169141825005195509)
XLA Ops:
  0.0 60.4 %shard_map.100.src = bf16[64,5120]{1,0:T(8,128)(2,1)S(1)} custom-call(bf16[64,5120]{1,0:T(8,128)(2,1)} %hid_h.1, bf16[5120,1024]{1,0:T(8,128)(2,1)} %wq_h.1, bf16[5120,256]{1,0:T(8,128)(2,1)} %wk_h.1, bf16[5120,256]{1,0:T(8,128)(2,1)} %wv_h.1, bf16[1024,5120]{1,0:T(8,128)(2,1)} %wo_h.1, bf16[2048,128]{1,0:T(8,128)(2,1)} %bitcast.6, ...), custom_call_target="tpu_custom_call" | custom-call | tf_op jit(solution)/shard_map/pallas_call | solution.py:522
  60.4 0.8 %shard_map.101 = bf16[64,5120]{1,0:T(8,128)(2,1)} custom-call(bf16[64,5120]{1,0:T(8,128)(2,1)S(1)} %shard_map.100.src), custom_call_target="tpu_custom_call" | custom-call | tf_op jit(solution)/shard_map/pallas_call | solution.py:532
